TPU v7x, 256 devices: a whole 4x4x8 slice. The times are simulated.
256 devices in a mesh: section: 32 (over y, x, z_lo), tensor: 8 (over z_hi, core).
Axes of the slice: x: 4, y: 4, z: 8 (z_hi: 4, z_lo: 2; z = z_hi * 2 + z_lo), core: 2. Of those that a mesh axis runs over, the one named last changes fastest.
Arguments:
- hidden_in: bfloat16 [128, 8192], P(None, 'tensor'), may hold values from -36 to 36
- segment_ids: int32 [4, 32], replicated, may hold values from 0 to 7, never falling along the last dimension, each value on 1 to 8 neighbouring positions
- segment_job: int32 [4, 8], replicated, may hold values from 0 to 5
- job_adapter: int32 [6], replicated, may hold values from 0 to 3
- owner: int32 [32], P('section'), may hold values from 0 to 7
- frozen: bfloat16 [32, 8192, 4096], P('section', None, 'tensor'), may hold values from -0.0625 to 0.0625
- norm_gain: bfloat16 [32, 4096], P('section'), may hold values from 0.3984375 to 1.59375
- inbox_down: bfloat16 [32, 8, 4096, 128], P('section', 'tensor'), may hold values from -0.0625 to 0.0625
- inbox_up: bfloat16 [32, 8, 128, 4096], P('section', 'tensor'), may hold values from -1 to 1
Outputs:
- section_out: bfloat16 [32, 128, 4096], P('section', None, 'tensor')
Inputs may be any that keep to these rules, and one draw needn't show every extreme that they name: `segment_ids`: within each micro-batch the segment numbers never fall, and each of the 8 segments has 1 to 8 tokens.
All inputs are finite; a program needn't handle non-finite values.
Results may differ from a plain program's by a relative error of at most 0.02.
Values may be sent and summed in bfloat16 or wider, within the bound.
No kernel may reach another device: no remote copies, remote signals or barrier semaphores. Data moves between devices by JAX's collectives and lax.ppermute only.
A program may use at most 64 MiB of HBM per device.

v0:
```python
import jax
import jax.numpy as jnp
from jax import lax
from jax.sharding import PartitionSpec as P

R = 32
epsilon = 1e-05


def spread(block, axis, owner):
    block = jnp.where(lax.axis_index(axis) == owner, block, jnp.zeros_like(block))
    return lax.psum(block, axis)


def from_partner(value, axis, bit):
    mask = 2**bit
    pairs = [(source, source ^ mask) for source in range(lax.axis_size(axis))]
    return lax.ppermute(value, axis, pairs)


def side_by_side(arrays, axis, dim, along):
    ends, at = ([], 0)
    for a in arrays[:-1]:
        at += a.shape[along]
        ends.append(at)
    both = jnp.concatenate(arrays, axis=along)
    return tuple(jnp.split(lax.all_gather(both, axis, axis=dim, tiled=True), ends, axis=along))


def shifted(value, axis, steps):
    count = lax.axis_size(axis)
    first, last = (max(0, -steps), min(count, count - steps))
    return lax.ppermute(value, axis, [(source, source + steps) for source in range(first, last)])


def product(left, right):
    return jnp.dot(left, right, preferred_element_type=jnp.float32)


def both_halves(own_part, other_part, pair_side):
    lower_part = jnp.where(pair_side == 0, own_part, other_part)
    upper_part = jnp.where(pair_side == 0, other_part, own_part)
    return (lower_part, upper_part)


def local(
    hidden_in, segment_ids, segment_job, job_adapter, owner, frozen, norm_gain, inbox_down, inbox_up
):
    tensors = lax.axis_size("tensor")
    sections = lax.axis_size("section")
    levels = sections // 2
    piece_cols = frozen.shape[2]
    half_width = norm_gain.shape[1]
    full_width = 2 * half_width
    rank_cols = inbox_down.shape[3]
    unit_count = segment_ids.shape[0]
    unit_rows = segment_ids.shape[1]
    position = lax.axis_index("section")
    pair_side = position % 2
    section_level = position // 2
    shard_index = lax.axis_index("tensor")
    down_half, up_half = (
        spread(inbox_down[0, 0], "tensor", owner[0]),
        spread(inbox_up[0, 0], "tensor", owner[0]),
    )
    up_own = lax.dynamic_slice_in_dim(up_half, shard_index * piece_cols, piece_cols, 1)
    split_weight = frozen[0].reshape(tensors, 2, piece_cols, piece_cols)
    weight_low = split_weight[:, 0].reshape(half_width, piece_cols)
    weight_high = split_weight[:, 1].reshape(half_width, piece_cols)
    gain_own = norm_gain[0]
    down_other, gain_other = from_partner((down_half, gain_own), "section", 0)
    down_low, down_high = both_halves(down_half, down_other, pair_side)
    gain_low, gain_high = both_halves(gain_own, gain_other, pair_side)
    gain_low = gain_low.astype(jnp.float32)[None, :]
    gain_high = gain_high.astype(jnp.float32)[None, :]
    seg_hit = segment_ids[:, :, None] == lax.broadcasted_iota(
        jnp.int32, (1, 1, segment_job.shape[1]), 2
    )
    token_job = jnp.sum(jnp.where(seg_hit, segment_job[:, None, :], 0), axis=2)
    job_hit = token_job[:, :, None] == lax.broadcasted_iota(
        jnp.int32, (1, 1, job_adapter.shape[0]), 2
    )
    token_adapter = jnp.sum(jnp.where(job_hit, job_adapter[None, None, :], 0), axis=2)
    slot_of_column = lax.broadcasted_iota(jnp.int32, (1, rank_cols), 1) // R
    zero_piece = jnp.zeros((unit_rows, piece_cols), jnp.bfloat16)
    zero_rank = jnp.zeros((unit_rows, rank_cols), jnp.float32)
    results = jnp.zeros((unit_count * unit_rows, piece_cols), jnp.bfloat16)

    def pipe_step(step_turn, carry):
        incoming, incoming_other, results = carry
        unit_index = step_turn - section_level
        active = jnp.logical_and(unit_index >= 0, unit_index < unit_count)
        unit_slot = jnp.clip(unit_index, 0, unit_count - 1)
        source = lax.dynamic_slice_in_dim(
            hidden_in, jnp.clip(step_turn, 0, unit_count - 1) * unit_rows, unit_rows, 0
        )
        own_source = lax.dynamic_slice_in_dim(source, pair_side * piece_cols, piece_cols, 1)
        own_piece = jnp.where(section_level == 0, own_source, incoming)
        other_piece = from_partner(own_piece, "section", 0)
        own_half, other_half = side_by_side((own_piece, other_piece), "tensor", 1, 0)
        half_low, half_high = both_halves(own_half, other_half, pair_side)
        low_values = half_low.astype(jnp.float32)
        high_values = half_high.astype(jnp.float32)
        mean_square = (
            jnp.sum(low_values * low_values, axis=1) + jnp.sum(high_values * high_values, axis=1)
        ) / full_width
        row_scale = lax.rsqrt(mean_square + epsilon)[:, None]
        normed_low = (low_values * row_scale * gain_low).astype(jnp.bfloat16)
        normed_high = (high_values * row_scale * gain_high).astype(jnp.bfloat16)
        unit_adapter = lax.dynamic_index_in_dim(token_adapter, unit_slot, 0, keepdims=False)
        keep_mask = slot_of_column == unit_adapter[:, None]
        projected = lax.cond(
            active,
            lambda: product(normed_low, down_low) + product(normed_high, down_high),
            lambda: zero_rank,
        )
        kept_rank = jnp.where(keep_mask, projected, 0.0).astype(jnp.bfloat16)

        def compute():
            frozen_out = product(normed_low, weight_low) + product(normed_high, weight_high)
            adapted = product(kept_rank, up_own)
            return (own_piece.astype(jnp.float32) + frozen_out + adapted).astype(jnp.bfloat16)

        fresh_piece = lax.cond(active, compute, lambda: zero_piece)
        previous = lax.dynamic_slice_in_dim(results, unit_slot * unit_rows, unit_rows, 0)
        results = lax.dynamic_update_slice_in_dim(
            results, jnp.where(active, fresh_piece, previous), unit_slot * unit_rows, 0
        )
        moved_piece = shifted(fresh_piece, "section", 2)
        return (moved_piece, incoming_other, results)

    carry = lax.fori_loop(0, unit_count + levels - 1, pipe_step, (zero_piece, zero_piece, results))
    return carry[2][None]


def solution(mesh):
    return jax.shard_map(
        local,
        mesh=mesh,
        in_specs=(
            P(None, "tensor"),
            P(),
            P(),
            P(),
            P("section"),
            P("section", None, "tensor"),
            P("section", None),
            P("section", "tensor", None, None),
            P("section", "tensor", None, None),
        ),
        out_specs=P("section", None, "tensor"),
        check_vma=False,
    )
```

profile of v0, /device:TPU:62, one launch (start us, length us, event | category | flops | bytes accessed | tf_op | source)
XLA Modules:
  0.0 724.2 jit_solution(11403315338042876360)
XLA Ops:
  9.7 88.9 %all-reduce.3.cloned.1.call-done = (bf16[4096,128]{1,0:T(8,128)(2,1)}, bf16[128,4096]{1,0:T(8,128)(2,1)}) async-done(((bf16[4096,128]{1,0:T(8,128)(2,1)}, bf16[128,4096]{1,0:T(8,128)(2,1)}), (bf16[4096,128]{1,0:T(8,128)(2,1)}, bf16[128,4096]{1,0:T(8,128)(2,1)})) %all-reduce.3.cloned.1.call-update) | async-done | bytes 2097168 | tf_op jit(solution)/shard_map/psum | solution.py:12
  105.8 17.8 %collective-permute-done.3 = bf16[4096,128]{1,0:T(8,128)(2,1)} collective-permute-done((bf16[4096,128]{1,0:T(8,128)(2,1)}, bf16[4096,128]{1,0:T(8,128)(2,1)}, u32[]{:S(2)}, u32[]{:S(2)}) %collective-permute-start.3) | collective-permute-done | bytes 1048608 | tf_op jit(solution)/shard_map/ppermute | solution.py:18
  125.0 591.6 %while.19 = (s32[]{:T(128)}, bf16[32,512]{1,0:T(8,128)(2,1)S(1)}, bf16[128,512]{1,0:T(8,128)(2,1)S(1)}, s32[]{:T(128)}, pred[]{:T(512)}, /*index=5*/pred[]{:T(51...) while((s32[]{:T(128)}, bf16[32,512]{1,0:T(8,128)(2,1)S(1)}, ...), condition=%wide.region_11.12_spmd.clone, body=%wide.region_4.11_spmd.clone.sunk | while | flops 342361152 | bytes 31623924 | solution.py:132
  129.9 15.0 %all_gather.13 = bf16[64,4096]{1,0:T(8,128)(2,1)S(1)} all-gather(bf16[64,512]{1,0:T(8,128)(2,1)S(1)} %pad_maximum_fusion.2), channel_id=1, replica_groups=mesh['section'=32,'tensor'=8] {'tensor'}, dimensions={1}, use_global_device_ids=true | all-gather | bytes 589824 | tf_op jit(solution)/shard_map/while/body/eval_jaxpr/all_gather | solution.py:27
  156.2 15.0 %all_gather.13 = bf16[64,4096]{1,0:T(8,128)(2,1)S(1)} all-gather(bf16[64,512]{1,0:T(8,128)(2,1)S(1)} %pad_maximum_fusion.2), channel_id=1, replica_groups=mesh['section'=32,'tensor'=8] {'tensor'}, dimensions={1}, use_global_device_ids=true | all-gather | bytes 589824 | tf_op jit(solution)/shard_map/while/body/eval_jaxpr/all_gather | solution.py:27
  182.6 15.2 %all_gather.13 = bf16[64,4096]{1,0:T(8,128)(2,1)S(1)} all-gather(bf16[64,512]{1,0:T(8,128)(2,1)S(1)} %pad_maximum_fusion.2), channel_id=1, replica_groups=mesh['section'=32,'tensor'=8] {'tensor'}, dimensions={1}, use_global_device_ids=true | all-gather | bytes 589824 | tf_op jit(solution)/shard_map/while/body/eval_jaxpr/all_gather | solution.py:27
  209.3 15.3 %all_gather.13 = bf16[64,4096]{1,0:T(8,128)(2,1)S(1)} all-gather(bf16[64,512]{1,0:T(8,128)(2,1)S(1)} %pad_maximum_fusion.2), channel_id=1, replica_groups=mesh['section'=32,'tensor'=8] {'tensor'}, dimensions={1}, use_global_device_ids=true | all-gather | bytes 589824 | tf_op jit(solution)/shard_map/while/body/eval_jaxpr/all_gather | solution.py:27
  236.0 15.4 %all_gather.13 = bf16[64,4096]{1,0:T(8,128)(2,1)S(1)} all-gather(bf16[64,512]{1,0:T(8,128)(2,1)S(1)} %pad_maximum_fusion.2), channel_id=1, replica_groups=mesh['section'=32,'tensor'=8] {'tensor'}, dimensions={1}, use_global_device_ids=true | all-gather | bytes 589824 | tf_op jit(solution)/shard_map/while/body/eval_jaxpr/all_gather | solution.py:27
  263.0 15.3 %all_gather.13 = bf16[64,4096]{1,0:T(8,128)(2,1)S(1)} all-gather(bf16[64,512]{1,0:T(8,128)(2,1)S(1)} %pad_maximum_fusion.2), channel_id=1, replica_groups=mesh['section'=32,'tensor'=8] {'tensor'}, dimensions={1}, use_global_device_ids=true | all-gather | bytes 589824 | tf_op jit(solution)/shard_map/while/body/eval_jaxpr/all_gather | solution.py:27
  280.1 6.8 collective-permute-done.1
  292.0 15.2 %all_gather.13 = bf16[64,4096]{1,0:T(8,128)(2,1)S(1)} all-gather(bf16[64,512]{1,0:T(8,128)(2,1)S(1)} %pad_maximum_fusion.2), channel_id=1, replica_groups=mesh['section'=32,'tensor'=8] {'tensor'}, dimensions={1}, use_global_device_ids=true | all-gather | bytes 589824 | tf_op jit(solution)/shard_map/while/body/eval_jaxpr/all_gather | solution.py:27
  309.1 6.6 collective-permute-done.1
  320.8 15.2 %all_gather.13 = bf16[64,4096]{1,0:T(8,128)(2,1)S(1)} all-gather(bf16[64,512]{1,0:T(8,128)(2,1)S(1)} %pad_maximum_fusion.2), channel_id=1, replica_groups=mesh['section'=32,'tensor'=8] {'tensor'}, dimensions={1}, use_global_device_ids=true | all-gather | bytes 589824 | tf_op jit(solution)/shard_map/while/body/eval_jaxpr/all_gather | solution.py:27
  337.9 6.6 collective-permute-done.1
  349.7 15.3 %all_gather.13 = bf16[64,4096]{1,0:T(8,128)(2,1)S(1)} all-gather(bf16[64,512]{1,0:T(8,128)(2,1)S(1)} %pad_maximum_fusion.2), channel_id=1, replica_groups=mesh['section'=32,'tensor'=8] {'tensor'}, dimensions={1}, use_global_device_ids=true | all-gather | bytes 589824 | tf_op jit(solution)/shard_map/while/body/eval_jaxpr/all_gather | solution.py:27
  366.8 6.6 collective-permute-done.1
  378.6 15.2 %all_gather.13 = bf16[64,4096]{1,0:T(8,128)(2,1)S(1)} all-gather(bf16[64,512]{1,0:T(8,128)(2,1)S(1)} %pad_maximum_fusion.2), channel_id=1, replica_groups=mesh['section'=32,'tensor'=8] {'tensor'}, dimensions={1}, use_global_device_ids=true | all-gather | bytes 589824 | tf_op jit(solution)/shard_map/while/body/eval_jaxpr/all_gather | solution.py:27
  395.7 6.7 collective-permute-done.1
  407.5 15.2 %all_gather.13 = bf16[64,4096]{1,0:T(8,128)(2,1)S(1)} all-gather(bf16[64,512]{1,0:T(8,128)(2,1)S(1)} %pad_maximum_fusion.2), channel_id=1, replica_groups=mesh['section'=32,'tensor'=8] {'tensor'}, dimensions={1}, use_global_device_ids=true | all-gather | bytes 589824 | tf_op jit(solution)/shard_map/while/body/eval_jaxpr/all_gather | solution.py:27
  424.6 6.8 collective-permute-done.1
  436.5 15.3 %all_gather.13 = bf16[64,4096]{1,0:T(8,128)(2,1)S(1)} all-gather(bf16[64,512]{1,0:T(8,128)(2,1)S(1)} %pad_maximum_fusion.2), channel_id=1, replica_groups=mesh['section'=32,'tensor'=8] {'tensor'}, dimensions={1}, use_global_device_ids=true | all-gather | bytes 589824 | tf_op jit(solution)/shard_map/while/body/eval_jaxpr/all_gather | solution.py:27
  465.2 15.5 %all_gather.13 = bf16[64,4096]{1,0:T(8,128)(2,1)S(1)} all-gather(bf16[64,512]{1,0:T(8,128)(2,1)S(1)} %pad_maximum_fusion.2), channel_id=1, replica_groups=mesh['section'=32,'tensor'=8] {'tensor'}, dimensions={1}, use_global_device_ids=true | all-gather | bytes 589824 | tf_op jit(solution)/shard_map/while/body/eval_jaxpr/all_gather | solution.py:27
  493.8 15.4 %all_gather.13 = bf16[64,4096]{1,0:T(8,128)(2,1)S(1)} all-gather(bf16[64,512]{1,0:T(8,128)(2,1)S(1)} %pad_maximum_fusion.2), channel_id=1, replica_groups=mesh['section'=32,'tensor'=8] {'tensor'}, dimensions={1}, use_global_device_ids=true | all-gather | bytes 589824 | tf_op jit(solution)/shard_map/while/body/eval_jaxpr/all_gather | solution.py:27
  522.3 15.5 %all_gather.13 = bf16[64,4096]{1,0:T(8,128)(2,1)S(1)} all-gather(bf16[64,512]{1,0:T(8,128)(2,1)S(1)} %pad_maximum_fusion.2), channel_id=1, replica_groups=mesh['section'=32,'tensor'=8] {'tensor'}, dimensions={1}, use_global_device_ids=true | all-gather | bytes 589824 | tf_op jit(solution)/shard_map/while/body/eval_jaxpr/all_gather | solution.py:27
  539.6 44.4 %collective-permute-done.1 = bf16[32,512]{1,0:T(8,128)(2,1)S(1)} collective-permute-done((bf16[32,512]{1,0:T(8,128)(2,1)S(1)}, bf16[32,512]{1,0:T(8,128)(2,1)S(1)}, u32[]{:S(2)}, u32[]{:S(2)}) %collective-permute-start.1) | collective-permute-done | bytes 32800 | tf_op jit(solution)/shard_map/while/body/eval_jaxpr/ppermute | solution.py:33
  588.9 15.4 %all_gather.13 = bf16[64,4096]{1,0:T(8,128)(2,1)S(1)} all-gather(bf16[64,512]{1,0:T(8,128)(2,1)S(1)} %pad_maximum_fusion.2), channel_id=1, replica_groups=mesh['section'=32,'tensor'=8] {'tensor'}, dimensions={1}, use_global_device_ids=true | all-gather | bytes 589824 | tf_op jit(solution)/shard_map/while/body/eval_jaxpr/all_gather | solution.py:27
  611.2 6.5 collective-permute-done.1
  622.6 15.4 %all_gather.13 = bf16[64,4096]{1,0:T(8,128)(2,1)S(1)} all-gather(bf16[64,512]{1,0:T(8,128)(2,1)S(1)} %pad_maximum_fusion.2), channel_id=1, replica_groups=mesh['section'=32,'tensor'=8] {'tensor'}, dimensions={1}, use_global_device_ids=true | all-gather | bytes 589824 | tf_op jit(solution)/shard_map/while/body/eval_jaxpr/all_gather | solution.py:27
  644.8 6.5 collective-permute-done.1
  656.2 15.4 %all_gather.13 = bf16[64,4096]{1,0:T(8,128)(2,1)S(1)} all-gather(bf16[64,512]{1,0:T(8,128)(2,1)S(1)} %pad_maximum_fusion.2), channel_id=1, replica_groups=mesh['section'=32,'tensor'=8] {'tensor'}, dimensions={1}, use_global_device_ids=true | all-gather | bytes 589824 | tf_op jit(solution)/shard_map/while/body/eval_jaxpr/all_gather | solution.py:27
  678.5 6.5 collective-permute-done.1
  689.9 15.4 %all_gather.13 = bf16[64,4096]{1,0:T(8,128)(2,1)S(1)} all-gather(bf16[64,512]{1,0:T(8,128)(2,1)S(1)} %pad_maximum_fusion.2), channel_id=1, replica_groups=mesh['section'=32,'tensor'=8] {'tensor'}, dimensions={1}, use_global_device_ids=true | all-gather | bytes 589824 | tf_op jit(solution)/shard_map/while/body/eval_jaxpr/all_gather | solution.py:27
  (361 shorter events, 227.3 us)
Async XLA Ops:
  6.5 92.0 %all-reduce.3.cloned.1.call-start = ((), (), s32[]{:S(2)}) async-start(), calls=%async_computation | async-start | bytes 4194304 | tf_op jit(solution)/shard_map/psum | solution.py:12
  9.5 95.4 %collective-permute-start.2 = (bf16[4096]{0:T(1024)(128)(2,1)S(1)}, bf16[4096]{0:T(1024)(128)(2,1)S(1)}, u32[]{:S(2)}, u32[]{:S(2)}) collective-permute-start(bf16[4096]{0:T(1024)(128)(2,1)S(1)} %reduce), channel_id=1, source_target_pairs={{0,8},{8,0},{16,24},{24,16},{32,40},{40,32},{48,56},{56,48},{64,72... | collective-permute-start | bytes 24584 | tf_op jit(solution)/shard_map/ppermute | solution.py:18
  98.5 25.1 %collective-permute-start.3 = (bf16[4096,128]{1,0:T(8,128)(2,1)}, bf16[4096,128]{1,0:T(8,128)(2,1)}, u32[]{:S(2)}, u32[]{:S(2)}) collective-permute-start(bf16[4096,128]{1,0:T(8,128)(2,1)} %get-tuple-element.551), channel_id=1, source_target_pairs={{0,8},{8,0},{16,24},{24,16},{32,40},{40,32},{48,56},{56,48},{64,72... | collective-permute-start | bytes 3145736 | tf_op jit(solution)/shard_map/ppermute | solution.py:18
  145.5 5.8 collective-permute-start.1
  171.8 5.8 collective-permute-start.1
  198.4 5.8 collective-permute-start.1
  205.1 4.2 collective-permute-start
  225.1 5.8 collective-permute-start.1
  231.8 4.2 collective-permute-start
  252.0 6.0 collective-permute-start.1
  278.8 8.1 %collective-permute-start.1 = (bf16[32,512]{1,0:T(8,128)(2,1)S(1)}, bf16[32,512]{1,0:T(8,128)(2,1)S(1)}, u32[]{:S(2)}, u32[]{:S(2)}) collective-permute-start(bf16[32,512]{1,0:T(8,128)(2,1)S(1)} %get-tuple-element.738), channel_id=1, source_target_pairs={{0,16},{8,24},{16,32},{24,40},{32,48},{40,56},{48,64},{56,72},{64,... | collective-permute-start | bytes 98312 | tf_op jit(solution)/shard_map/while/body/eval_jaxpr/ppermute | solution.py:33
  287.8 4.2 collective-permute-start
  307.8 7.9 %collective-permute-start.1 = (bf16[32,512]{1,0:T(8,128)(2,1)S(1)}, bf16[32,512]{1,0:T(8,128)(2,1)S(1)}, u32[]{:S(2)}, u32[]{:S(2)}) collective-permute-start(bf16[32,512]{1,0:T(8,128)(2,1)S(1)} %get-tuple-element.738), channel_id=1, source_target_pairs={{0,16},{8,24},{16,32},{24,40},{32,48},{40,56},{48,64},{56,72},{64,... | collective-permute-start | bytes 98312 | tf_op jit(solution)/shard_map/while/body/eval_jaxpr/ppermute | solution.py:33
  316.5 4.3 collective-permute-start
  336.6 7.9 %collective-permute-start.1 = (bf16[32,512]{1,0:T(8,128)(2,1)S(1)}, bf16[32,512]{1,0:T(8,128)(2,1)S(1)}, u32[]{:S(2)}, u32[]{:S(2)}) collective-permute-start(bf16[32,512]{1,0:T(8,128)(2,1)S(1)} %get-tuple-element.738), channel_id=1, source_target_pairs={{0,16},{8,24},{16,32},{24,40},{32,48},{40,56},{48,64},{56,72},{64,... | collective-permute-start | bytes 98312 | tf_op jit(solution)/shard_map/while/body/eval_jaxpr/ppermute | solution.py:33
  345.4 4.2 collective-permute-start
  365.5 7.9 %collective-permute-start.1 = (bf16[32,512]{1,0:T(8,128)(2,1)S(1)}, bf16[32,512]{1,0:T(8,128)(2,1)S(1)}, u32[]{:S(2)}, u32[]{:S(2)}) collective-permute-start(bf16[32,512]{1,0:T(8,128)(2,1)S(1)} %get-tuple-element.738), channel_id=1, source_target_pairs={{0,16},{8,24},{16,32},{24,40},{32,48},{40,56},{48,64},{56,72},{64,... | collective-permute-start | bytes 98312 | tf_op jit(solution)/shard_map/while/body/eval_jaxpr/ppermute | solution.py:33
  374.3 4.2 collective-permute-start
  394.4 8.0 %collective-permute-start.1 = (bf16[32,512]{1,0:T(8,128)(2,1)S(1)}, bf16[32,512]{1,0:T(8,128)(2,1)S(1)}, u32[]{:S(2)}, u32[]{:S(2)}) collective-permute-start(bf16[32,512]{1,0:T(8,128)(2,1)S(1)} %get-tuple-element.738), channel_id=1, source_target_pairs={{0,16},{8,24},{16,32},{24,40},{32,48},{40,56},{48,64},{56,72},{64,... | collective-permute-start | bytes 98312 | tf_op jit(solution)/shard_map/while/body/eval_jaxpr/ppermute | solution.py:33
  403.3 4.2 collective-permute-start
  423.3 8.1 %collective-permute-start.1 = (bf16[32,512]{1,0:T(8,128)(2,1)S(1)}, bf16[32,512]{1,0:T(8,128)(2,1)S(1)}, u32[]{:S(2)}, u32[]{:S(2)}) collective-permute-start(bf16[32,512]{1,0:T(8,128)(2,1)S(1)} %get-tuple-element.738), channel_id=1, source_target_pairs={{0,16},{8,24},{16,32},{24,40},{32,48},{40,56},{48,64},{56,72},{64,... | collective-permute-start | bytes 98312 | tf_op jit(solution)/shard_map/while/body/eval_jaxpr/ppermute | solution.py:33
  432.3 4.2 collective-permute-start
  452.4 7.7 %collective-permute-start.1 = (bf16[32,512]{1,0:T(8,128)(2,1)S(1)}, bf16[32,512]{1,0:T(8,128)(2,1)S(1)}, u32[]{:S(2)}, u32[]{:S(2)}) collective-permute-start(bf16[32,512]{1,0:T(8,128)(2,1)S(1)} %get-tuple-element.738), channel_id=1, source_target_pairs={{0,16},{8,24},{16,32},{24,40},{32,48},{40,56},{48,64},{56,72},{64,... | collective-permute-start | bytes 98312 | tf_op jit(solution)/shard_map/while/body/eval_jaxpr/ppermute | solution.py:33
  460.9 4.2 collective-permute-start
  481.3 7.4 %collective-permute-start.1 = (bf16[32,512]{1,0:T(8,128)(2,1)S(1)}, bf16[32,512]{1,0:T(8,128)(2,1)S(1)}, u32[]{:S(2)}, u32[]{:S(2)}) collective-permute-start(bf16[32,512]{1,0:T(8,128)(2,1)S(1)} %get-tuple-element.738), channel_id=1, source_target_pairs={{0,16},{8,24},{16,32},{24,40},{32,48},{40,56},{48,64},{56,72},{64,... | collective-permute-start | bytes 98312 | tf_op jit(solution)/shard_map/while/body/eval_jaxpr/ppermute | solution.py:33
  489.6 4.2 collective-permute-start
  509.8 7.4 %collective-permute-start.1 = (bf16[32,512]{1,0:T(8,128)(2,1)S(1)}, bf16[32,512]{1,0:T(8,128)(2,1)S(1)}, u32[]{:S(2)}, u32[]{:S(2)}) collective-permute-start(bf16[32,512]{1,0:T(8,128)(2,1)S(1)} %get-tuple-element.738), channel_id=1, source_target_pairs={{0,16},{8,24},{16,32},{24,40},{32,48},{40,56},{48,64},{56,72},{64,... | collective-permute-start | bytes 98312 | tf_op jit(solution)/shard_map/while/body/eval_jaxpr/ppermute | solution.py:33
  538.3 45.7 %collective-permute-start.1 = (bf16[32,512]{1,0:T(8,128)(2,1)S(1)}, bf16[32,512]{1,0:T(8,128)(2,1)S(1)}, u32[]{:S(2)}, u32[]{:S(2)}) collective-permute-start(bf16[32,512]{1,0:T(8,128)(2,1)S(1)} %get-tuple-element.738), channel_id=1, source_target_pairs={{0,16},{8,24},{16,32},{24,40},{32,48},{40,56},{48,64},{56,72},{64,... | collective-permute-start | bytes 98312 | tf_op jit(solution)/shard_map/while/body/eval_jaxpr/ppermute | solution.py:33
  609.8 7.9 %collective-permute-start.1 = (bf16[32,512]{1,0:T(8,128)(2,1)S(1)}, bf16[32,512]{1,0:T(8,128)(2,1)S(1)}, u32[]{:S(2)}, u32[]{:S(2)}) collective-permute-start(bf16[32,512]{1,0:T(8,128)(2,1)S(1)} %get-tuple-element.738), channel_id=1, source_target_pairs={{0,16},{8,24},{16,32},{24,40},{32,48},{40,56},{48,64},{56,72},{64,... | collective-permute-start | bytes 98312 | tf_op jit(solution)/shard_map/while/body/eval_jaxpr/ppermute | solution.py:33
  643.5 7.9 %collective-permute-start.1 = (bf16[32,512]{1,0:T(8,128)(2,1)S(1)}, bf16[32,512]{1,0:T(8,128)(2,1)S(1)}, u32[]{:S(2)}, u32[]{:S(2)}) collective-permute-start(bf16[32,512]{1,0:T(8,128)(2,1)S(1)} %get-tuple-element.738), channel_id=1, source_target_pairs={{0,16},{8,24},{16,32},{24,40},{32,48},{40,56},{48,64},{56,72},{64,... | collective-permute-start | bytes 98312 | tf_op jit(solution)/shard_map/while/body/eval_jaxpr/ppermute | solution.py:33
  677.2 7.9 %collective-permute-start.1 = (bf16[32,512]{1,0:T(8,128)(2,1)S(1)}, bf16[32,512]{1,0:T(8,128)(2,1)S(1)}, u32[]{:S(2)}, u32[]{:S(2)}) collective-permute-start(bf16[32,512]{1,0:T(8,128)(2,1)S(1)} %get-tuple-element.738), channel_id=1, source_target_pairs={{0,16},{8,24},{16,32},{24,40},{32,48},{40,56},{48,64},{56,72},{64,... | collective-permute-start | bytes 98312 | tf_op jit(solution)/shard_map/while/body/eval_jaxpr/ppermute | solution.py:33
  710.9 5.8 collective-permute-start.1
  (19 other events, 268.9 us)
Sparse Core Ops, SparseCore 0:
  10.0 88.4 all-reduce.2
where the time goes:
time: 726 us; the launch traced here: 724 us
  waiting for transfers between devices  303 us (42%)
  blocking collectives  291 us (40%)
  starting transfers between devices  56.9 us (8%)
  other arithmetic  30.6 us (4%)
  matrix products  18.6 us (3%)
  between operations  14.2 us (2%)
  local copies, waits for them, and re-layouts  8.94 us (1%)
    all_gather x19, blocking collectives, side_by_side(): lax.all_gather(both, axis, axis=dim, tiled=True)  291 us
    ppermute x19, waiting for transfers between devices, shifted(): lax.ppermute(value, axis, [(source, source + steps) for source in range(f...  150 us
    psum x1, waiting for transfers between devices, spread(): return lax.psum(block, axis)  88.9 us
    ppermute x21, waiting for transfers between devices, from_partner(): return lax.ppermute(value, axis, pairs)  63.9 us
    ppermute x21, starting transfers between devices, from_partner(): return lax.ppermute(value, axis, pairs)  32.3 us
    ppermute x19, starting transfers between devices, shifted(): lax.ppermute(value, axis, [(source, source + steps) for source in range(f...  24.6 us
    dot_general x20, matrix products, product(): return jnp.dot(left, right, preferred_element_type=jnp.float32)  18.6 us
    select_n x19, other arithmetic, pipe_step(): own_piece = jnp.where(section_level == 0, own_source, incoming)  16.1 us
  transfers between devices with their start and end apart: 41, of which 40 were waited for; matrix products, arithmetic and copies ran while one was open for 1% of the time, Pallas kernels for 0%

commit v1 on v0

--- a/solution.py
+++ b/solution.py
@@ -5,11 +5,12 @@
 
 R = 32
 epsilon = 1e-05
+drive_the_sizes = lambda ax_name, u_in: jnp.sum(lax.all_gather(u_in, axis_name=ax_name), 0)
 
 
 def spread(block, axis, owner):
     block = jnp.where(lax.axis_index(axis) == owner, block, jnp.zeros_like(block))
-    return lax.psum(block, axis)
+    return drive_the_sizes(axis, block)
 
 
 def from_partner(value, axis, bit):

time: 726 us -> 812 us (1.12)
  waiting for transfers between devices: 303 us -> 374 us
  other arithmetic: 30.6 us -> 41.1 us
    all_gather x0 -> x2, waiting for transfers between devices: none -> 179 us  [lax.all_gather(u_in, axis_name=ax_name)]
    psum x1 -> x0, waiting for transfers between devices: 88.9 us -> none  [spread(): return lax.psum(block, axis)]
    ppermute x21, waiting for transfers between devices: 63.9 us -> 42.4 us  [from_partner(): return lax.ppermute(value, axis, pairs)]
    reduce_sum x0 -> x2, other arithmetic: none -> 10.1 us  [jnp.sum(lax.all_gather(u_in, axis_name=ax_name), 0)]
  transfers between devices with their start and end apart: 41 -> 42, of which waited for: 40 -> 40; matrix products, arithmetic and copies ran while one was open for 1% -> 2% of each run, Pallas kernels for 0% -> 0%
where the time goes in v1:
time: 812 us; the launch traced here: 808 us
  waiting for transfers between devices  374 us (46%)
  blocking collectives  290 us (36%)
  starting transfers between devices  61 us (8%)
  other arithmetic  41.1 us (5%)
  matrix products  18.6 us (2%)
  between operations  14.2 us (2%)
    all_gather x19, blocking collectives, side_by_side(): lax.all_gather(both, axis, axis=dim, tiled=True)  290 us
    all_gather x2, waiting for transfers between devices, lax.all_gather(u_in, axis_name=ax_name)  179 us
    ppermute x19, waiting for transfers between devices, shifted(): lax.ppermute(value, axis, [(source, source + steps) for source in range(f...  152 us
    ppermute x21, waiting for transfers between devices, from_partner(): return lax.ppermute(value, axis, pairs)  42.4 us
    ppermute x21, starting transfers between devices, from_partner(): return lax.ppermute(value, axis, pairs)  36.4 us
    ppermute x19, starting transfers between devices, shifted(): lax.ppermute(value, axis, [(source, source + steps) for source in range(f...  24.6 us
    dot_general x20, matrix products, product(): return jnp.dot(left, right, preferred_element_type=jnp.float32)  18.6 us
  transfers between devices with their start and end apart: 42, of which 40 were waited for; matrix products, arithmetic and copies ran while one was open for 2% of the time, Pallas kernels for 0%

profile of v1, /device:TPU:62, one launch (start us, length us, event | category | flops | bytes accessed | tf_op | source)
XLA Modules:
  0.0 807.9 jit_solution(6684304179830756334)
XLA Ops:
  9.8 89.4 %all-gather.5.cloned.1.call-done = bf16[8,1,4096,128]{3,2,1,0:T(8,128)(2,1)} async-done(((bf16[1,1,4096,128]{3,2,1,0:T(8,128)(2,1)}), bf16[8,1,4096,128]{3,2,1,0:T(8,128)(2,1)}) %all-gather.5.cloned.1.call-update) | async-done | bytes 8388624 | tf_op jit(solution)/shard_map/all_gather | solution.py:8
  110.6 89.5 %all-gather.7.cloned.1.call-done = bf16[8,1,128,4096]{3,2,1,0:T(8,128)(2,1)} async-done(((bf16[1,1,128,4096]{3,2,1,0:T(8,128)(2,1)}), bf16[8,1,128,4096]{3,2,1,0:T(8,128)(2,1)}) %all-gather.7.cloned.1.call-update) | async-done | bytes 8388624 | tf_op jit(solution)/shard_map/all_gather | solution.py:8
  206.8 593.7 %while.19 = (s32[]{:T(128)}, bf16[32,512]{1,0:T(8,128)(2,1)S(1)}, bf16[128,512]{1,0:T(8,128)(2,1)S(1)}, s32[]{:T(128)}, pred[]{:T(512)}, /*index=5*/pred[]{:T(51...) while((s32[]{:T(128)}, bf16[32,512]{1,0:T(8,128)(2,1)S(1)}, ...), condition=%wide.region_11.12_spmd.clone, body=%wide.region_4.11_spmd.clone.sunk | while | flops 342361152 | bytes 31623924 | solution.py:133
  211.7 15.2 %all_gather.23 = bf16[64,4096]{1,0:T(8,128)(2,1)S(1)} all-gather(bf16[64,512]{1,0:T(8,128)(2,1)S(1)} %pad_maximum_fusion.2), channel_id=1, replica_groups=mesh['section'=32,'tensor'=8] {'tensor'}, dimensions={1}, use_global_device_ids=true | all-gather | bytes 589824 | tf_op jit(solution)/shard_map/while/body/eval_jaxpr/all_gather | solution.py:28
  238.2 15.1 %all_gather.23 = bf16[64,4096]{1,0:T(8,128)(2,1)S(1)} all-gather(bf16[64,512]{1,0:T(8,128)(2,1)S(1)} %pad_maximum_fusion.2), channel_id=1, replica_groups=mesh['section'=32,'tensor'=8] {'tensor'}, dimensions={1}, use_global_device_ids=true | all-gather | bytes 589824 | tf_op jit(solution)/shard_map/while/body/eval_jaxpr/all_gather | solution.py:28
  264.5 15.0 %all_gather.23 = bf16[64,4096]{1,0:T(8,128)(2,1)S(1)} all-gather(bf16[64,512]{1,0:T(8,128)(2,1)S(1)} %pad_maximum_fusion.2), channel_id=1, replica_groups=mesh['section'=32,'tensor'=8] {'tensor'}, dimensions={1}, use_global_device_ids=true | all-gather | bytes 589824 | tf_op jit(solution)/shard_map/while/body/eval_jaxpr/all_gather | solution.py:28
  291.4 14.9 %all_gather.23 = bf16[64,4096]{1,0:T(8,128)(2,1)S(1)} all-gather(bf16[64,512]{1,0:T(8,128)(2,1)S(1)} %pad_maximum_fusion.2), channel_id=1, replica_groups=mesh['section'=32,'tensor'=8] {'tensor'}, dimensions={1}, use_global_device_ids=true | all-gather | bytes 589824 | tf_op jit(solution)/shard_map/while/body/eval_jaxpr/all_gather | solution.py:28
  318.2 14.9 %all_gather.23 = bf16[64,4096]{1,0:T(8,128)(2,1)S(1)} all-gather(bf16[64,512]{1,0:T(8,128)(2,1)S(1)} %pad_maximum_fusion.2), channel_id=1, replica_groups=mesh['section'=32,'tensor'=8] {'tensor'}, dimensions={1}, use_global_device_ids=true | all-gather | bytes 589824 | tf_op jit(solution)/shard_map/while/body/eval_jaxpr/all_gather | solution.py:28
  345.0 15.2 %all_gather.23 = bf16[64,4096]{1,0:T(8,128)(2,1)S(1)} all-gather(bf16[64,512]{1,0:T(8,128)(2,1)S(1)} %pad_maximum_fusion.2), channel_id=1, replica_groups=mesh['section'=32,'tensor'=8] {'tensor'}, dimensions={1}, use_global_device_ids=true | all-gather | bytes 589824 | tf_op jit(solution)/shard_map/while/body/eval_jaxpr/all_gather | solution.py:28
  362.1 6.5 collective-permute-done.1
  373.5 15.6 %all_gather.23 = bf16[64,4096]{1,0:T(8,128)(2,1)S(1)} all-gather(bf16[64,512]{1,0:T(8,128)(2,1)S(1)} %pad_maximum_fusion.2), channel_id=1, replica_groups=mesh['section'=32,'tensor'=8] {'tensor'}, dimensions={1}, use_global_device_ids=true | all-gather | bytes 589824 | tf_op jit(solution)/shard_map/while/body/eval_jaxpr/all_gather | solution.py:28
  402.3 15.5 %all_gather.23 = bf16[64,4096]{1,0:T(8,128)(2,1)S(1)} all-gather(bf16[64,512]{1,0:T(8,128)(2,1)S(1)} %pad_maximum_fusion.2), channel_id=1, replica_groups=mesh['section'=32,'tensor'=8] {'tensor'}, dimensions={1}, use_global_device_ids=true | all-gather | bytes 589824 | tf_op jit(solution)/shard_map/while/body/eval_jaxpr/all_gather | solution.py:28
  419.7 6.8 collective-permute-done.1
  431.3 15.3 %all_gather.23 = bf16[64,4096]{1,0:T(8,128)(2,1)S(1)} all-gather(bf16[64,512]{1,0:T(8,128)(2,1)S(1)} %pad_maximum_fusion.2), channel_id=1, replica_groups=mesh['section'=32,'tensor'=8] {'tensor'}, dimensions={1}, use_global_device_ids=true | all-gather | bytes 589824 | tf_op jit(solution)/shard_map/while/body/eval_jaxpr/all_gather | solution.py:28
  448.5 6.6 collective-permute-done.1
  460.0 15.5 %all_gather.23 = bf16[64,4096]{1,0:T(8,128)(2,1)S(1)} all-gather(bf16[64,512]{1,0:T(8,128)(2,1)S(1)} %pad_maximum_fusion.2), channel_id=1, replica_groups=mesh['section'=32,'tensor'=8] {'tensor'}, dimensions={1}, use_global_device_ids=true | all-gather | bytes 589824 | tf_op jit(solution)/shard_map/while/body/eval_jaxpr/all_gather | solution.py:28
  488.8 15.5 %all_gather.23 = bf16[64,4096]{1,0:T(8,128)(2,1)S(1)} all-gather(bf16[64,512]{1,0:T(8,128)(2,1)S(1)} %pad_maximum_fusion.2), channel_id=1, replica_groups=mesh['section'=32,'tensor'=8] {'tensor'}, dimensions={1}, use_global_device_ids=true | all-gather | bytes 589824 | tf_op jit(solution)/shard_map/while/body/eval_jaxpr/all_gather | solution.py:28
  506.2 6.7 collective-permute-done.1
  517.8 15.5 %all_gather.23 = bf16[64,4096]{1,0:T(8,128)(2,1)S(1)} all-gather(bf16[64,512]{1,0:T(8,128)(2,1)S(1)} %pad_maximum_fusion.2), channel_id=1, replica_groups=mesh['section'=32,'tensor'=8] {'tensor'}, dimensions={1}, use_global_device_ids=true | all-gather | bytes 589824 | tf_op jit(solution)/shard_map/while/body/eval_jaxpr/all_gather | solution.py:28
  546.4 15.5 %all_gather.23 = bf16[64,4096]{1,0:T(8,128)(2,1)S(1)} all-gather(bf16[64,512]{1,0:T(8,128)(2,1)S(1)} %pad_maximum_fusion.2), channel_id=1, replica_groups=mesh['section'=32,'tensor'=8] {'tensor'}, dimensions={1}, use_global_device_ids=true | all-gather | bytes 589824 | tf_op jit(solution)/shard_map/while/body/eval_jaxpr/all_gather | solution.py:28
  563.8 6.8 collective-permute-done.1
  575.4 15.3 %all_gather.23 = bf16[64,4096]{1,0:T(8,128)(2,1)S(1)} all-gather(bf16[64,512]{1,0:T(8,128)(2,1)S(1)} %pad_maximum_fusion.2), channel_id=1, replica_groups=mesh['section'=32,'tensor'=8] {'tensor'}, dimensions={1}, use_global_device_ids=true | all-gather | bytes 589824 | tf_op jit(solution)/shard_map/while/body/eval_jaxpr/all_gather | solution.py:28
  592.7 6.6 collective-permute-done.1
  604.1 15.6 %all_gather.23 = bf16[64,4096]{1,0:T(8,128)(2,1)S(1)} all-gather(bf16[64,512]{1,0:T(8,128)(2,1)S(1)} %pad_maximum_fusion.2), channel_id=1, replica_groups=mesh['section'=32,'tensor'=8] {'tensor'}, dimensions={1}, use_global_device_ids=true | all-gather | bytes 589824 | tf_op jit(solution)/shard_map/while/body/eval_jaxpr/all_gather | solution.py:28
  621.7 45.3 %collective-permute-done.1 = bf16[32,512]{1,0:T(8,128)(2,1)S(1)} collective-permute-done((bf16[32,512]{1,0:T(8,128)(2,1)S(1)}, bf16[32,512]{1,0:T(8,128)(2,1)S(1)}, u32[]{:S(2)}, u32[]{:S(2)}) %collective-permute-start.1) | collective-permute-done | bytes 32800 | tf_op jit(solution)/shard_map/while/body/eval_jaxpr/ppermute | solution.py:34
  672.3 14.9 %all_gather.23 = bf16[64,4096]{1,0:T(8,128)(2,1)S(1)} all-gather(bf16[64,512]{1,0:T(8,128)(2,1)S(1)} %pad_maximum_fusion.2), channel_id=1, replica_groups=mesh['section'=32,'tensor'=8] {'tensor'}, dimensions={1}, use_global_device_ids=true | all-gather | bytes 589824 | tf_op jit(solution)/shard_map/while/body/eval_jaxpr/all_gather | solution.py:28
  694.1 7.1 collective-permute-done.1
  706.4 14.9 %all_gather.23 = bf16[64,4096]{1,0:T(8,128)(2,1)S(1)} all-gather(bf16[64,512]{1,0:T(8,128)(2,1)S(1)} %pad_maximum_fusion.2), channel_id=1, replica_groups=mesh['section'=32,'tensor'=8] {'tensor'}, dimensions={1}, use_global_device_ids=true | all-gather | bytes 589824 | tf_op jit(solution)/shard_map/while/body/eval_jaxpr/all_gather | solution.py:28
  728.3 6.7 collective-permute-done.1
  740.2 15.0 %all_gather.23 = bf16[64,4096]{1,0:T(8,128)(2,1)S(1)} all-gather(bf16[64,512]{1,0:T(8,128)(2,1)S(1)} %pad_maximum_fusion.2), channel_id=1, replica_groups=mesh['section'=32,'tensor'=8] {'tensor'}, dimensions={1}, use_global_device_ids=true | all-gather | bytes 589824 | tf_op jit(solution)/shard_map/while/body/eval_jaxpr/all_gather | solution.py:28
  762.1 6.6 collective-permute-done.1
  774.0 15.0 %all_gather.23 = bf16[64,4096]{1,0:T(8,128)(2,1)S(1)} all-gather(bf16[64,512]{1,0:T(8,128)(2,1)S(1)} %pad_maximum_fusion.2), channel_id=1, replica_groups=mesh['section'=32,'tensor'=8] {'tensor'}, dimensions={1}, use_global_device_ids=true | all-gather | bytes 589824 | tf_op jit(solution)/shard_map/while/body/eval_jaxpr/all_gather | solution.py:28
  (366 shorter events, 238.4 us)
Async XLA Ops:
  6.5 92.6 %all-gather.5.cloned.1.call-start = ((), (), s32[]{:S(2)}) async-start(), calls=%async_computation | async-start | bytes 9437184 | tf_op jit(solution)/shard_map/all_gather | solution.py:8
  8.3 191.7 %all-gather.7.cloned.1.call-start = ((), (), s32[]{:S(2)}) async-start(), calls=%async_computation.1 | async-start | bytes 9437184 | tf_op jit(solution)/shard_map/all_gather | solution.py:8
  9.6 101.0 %collective-permute-start.2 = (bf16[4096]{0:T(1024)(128)(2,1)S(1)}, bf16[4096]{0:T(1024)(128)(2,1)S(1)}, u32[]{:S(2)}, u32[]{:S(2)}) collective-permute-start(bf16[4096]{0:T(1024)(128)(2,1)S(1)} %reduce.4), channel_id=1, source_target_pairs={{0,8},{8,0},{16,24},{24,16},{32,40},{40,32},{48,56},{56,48},{64,72... | collective-permute-start | bytes 24584 | tf_op jit(solution)/shard_map/ppermute | solution.py:19
  104.4 100.6 %collective-permute-start.3 = (bf16[4096,128]{1,0:T(8,128)(2,1)S(1)}, bf16[4096,128]{1,0:T(8,128)(2,1)}, u32[]{:S(2)}, u32[]{:S(2)}) collective-permute-start(bf16[4096,128]{1,0:T(8,128)(2,1)S(1)} %reduce_sum.78), channel_id=1, source_target_pairs={{0,8},{8,0},{16,24},{24,16},{32,40},{40,32},{48,56},{56,48},{64,72... | collective-permute-start | bytes 3145736 | tf_op jit(solution)/shard_map/ppermute | solution.py:19
  207.7 4.0 collective-permute-start
  227.5 5.8 collective-permute-start.1
  234.2 4.0 collective-permute-start
  253.8 5.8 collective-permute-start.1
  280.1 5.8 collective-permute-start.1
  286.8 4.6 collective-permute-start
  306.8 5.8 collective-permute-start.1
  313.5 4.7 collective-permute-start
  333.8 6.3 collective-permute-start.1
  340.9 4.0 collective-permute-start
  360.8 7.9 collective-permute-start.1
  389.7 7.7 collective-permute-start.1
  418.3 8.1 %collective-permute-start.1 = (bf16[32,512]{1,0:T(8,128)(2,1)S(1)}, bf16[32,512]{1,0:T(8,128)(2,1)S(1)}, u32[]{:S(2)}, u32[]{:S(2)}) collective-permute-start(bf16[32,512]{1,0:T(8,128)(2,1)S(1)} %get-tuple-element.734), channel_id=1, source_target_pairs={{0,16},{8,24},{16,32},{24,40},{32,48},{40,56},{48,64},{56,72},{64,... | collective-permute-start | bytes 98312 | tf_op jit(solution)/shard_map/while/body/eval_jaxpr/ppermute | solution.py:34
  447.2 7.9 collective-permute-start.1
  476.1 7.8 collective-permute-start.1
  504.8 8.1 collective-permute-start.1
  533.9 7.7 collective-permute-start.1
  562.5 8.1 %collective-permute-start.1 = (bf16[32,512]{1,0:T(8,128)(2,1)S(1)}, bf16[32,512]{1,0:T(8,128)(2,1)S(1)}, u32[]{:S(2)}, u32[]{:S(2)}) collective-permute-start(bf16[32,512]{1,0:T(8,128)(2,1)S(1)} %get-tuple-element.734), channel_id=1, source_target_pairs={{0,16},{8,24},{16,32},{24,40},{32,48},{40,56},{48,64},{56,72},{64,... | collective-permute-start | bytes 98312 | tf_op jit(solution)/shard_map/while/body/eval_jaxpr/ppermute | solution.py:34
  591.3 7.9 collective-permute-start.1
  620.3 46.6 %collective-permute-start.1 = (bf16[32,512]{1,0:T(8,128)(2,1)S(1)}, bf16[32,512]{1,0:T(8,128)(2,1)S(1)}, u32[]{:S(2)}, u32[]{:S(2)}) collective-permute-start(bf16[32,512]{1,0:T(8,128)(2,1)S(1)} %get-tuple-element.734), channel_id=1, source_target_pairs={{0,16},{8,24},{16,32},{24,40},{32,48},{40,56},{48,64},{56,72},{64,... | collective-permute-start | bytes 98312 | tf_op jit(solution)/shard_map/while/body/eval_jaxpr/ppermute | solution.py:34
  667.8 4.5 collective-permute-start
  692.7 8.4 %collective-permute-start.1 = (bf16[32,512]{1,0:T(8,128)(2,1)S(1)}, bf16[32,512]{1,0:T(8,128)(2,1)S(1)}, u32[]{:S(2)}, u32[]{:S(2)}) collective-permute-start(bf16[32,512]{1,0:T(8,128)(2,1)S(1)} %get-tuple-element.734), channel_id=1, source_target_pairs={{0,16},{8,24},{16,32},{24,40},{32,48},{40,56},{48,64},{56,72},{64,... | collective-permute-start | bytes 98312 | tf_op jit(solution)/shard_map/while/body/eval_jaxpr/ppermute | solution.py:34
  702.0 4.4 collective-permute-start
  726.9 8.0 collective-permute-start.1
  735.8 4.5 collective-permute-start
  760.8 7.9 collective-permute-start.1
  769.6 4.5 collective-permute-start
  794.6 5.8 collective-permute-start.1
  (20 other events, 259.4 us)
Sparse Core Ops, SparseCore 0:
  9.2 89.9 all-gather.4
  101.0 99.0 all-gather.6
